TPU v7x, 32 devices: a whole 2x2x4 slice. The times are simulated.
32 devices in a mesh: dp: 8 (over z, core), expert: 4 (over y, x).
Axes of the slice: x: 2, y: 2, z: 4, core: 2. Of those that a mesh axis runs over, the one named last changes fastest.
Arguments:
- attention_gradient: bfloat16 [8, 6144, 1024], P('dp', None, 'expert')
- attention_weight: float32 [6144, 1024], P('dp', 'expert'), may hold values from -6 to 6
- attention_mean: float32 [6144, 1024], P('dp', 'expert'), may hold values from -0.0012 to 0.0012
- attention_square: float32 [6144, 1024], P('dp', 'expert'), may hold values from 1e-09 to 1e-07
- expert_gradient: float32 [8, 4, 8, 6144], P('dp', 'expert')
- expert_weight: float32 [8, 4, 8, 6144], P('dp', 'expert'), may hold values from -6 to 6
- held_mean: float32 [8, 32, 6144], P('dp', 'expert'), may hold values from -0.0006 to 0.0006
- held_square: float32 [8, 32, 6144], P('dp', 'expert'), may hold values from 1e-10 to 1e-08
- live_block_count: int32 [4], replicated, may hold values from 1 to 8, as said below
- holder_table: int32 [4, 8], replicated, may hold values from 0 to 3, as said below
- slot_table: int32 [4, 8], replicated, may hold values from 0 to 7, as said below
- step_count: int32 [1], replicated, may hold values from 1 to 40
Outputs:
- updated_attention: float32 [6144, 1024], P('dp', 'expert')
- updated_means: float32 [6144, 1024], P('dp', 'expert')
- updated_squares: float32 [6144, 1024], P('dp', 'expert')
- updated_experts: float32 [8, 4, 8, 6144], P('dp', 'expert')
- expert_means: float32 [8, 4, 8, 6144], P('dp', 'expert')
- expert_squares: float32 [8, 4, 8, 6144], P('dp', 'expert')
Inputs may be any that keep to these rules, and one draw needn't show every extreme that they name: `live_block_count`: every expert has 1 to 8 live blocks and some expert has exactly 8. `holder_table`: no holder holds more than 2 live blocks of one expert, and some holder holds exactly 2 of one. `slot_table`: the blocks on one holder sit in distinct slots, and some holder has all 8 slots live.
All inputs are finite; a program needn't handle non-finite values.
Results may differ from a plain program's by a relative error of at most 0.0003.
Values sent between devices are 32-bit elements; how exact they have to be, the bound alone decides.
A program may use at most 64 MiB of HBM per device.

v0:
```python
import jax
import jax.numpy as jnp
from jax import lax
from jax.sharding import PartitionSpec as P

MAXB = 8
HSLOTS = 8
beta_first = 0.9
beta_second = 0.95
learn_rate = 0.1
decay_rate = 0.1
adam_epsilon = 1e-08
clip_norm = 1.0


def adam_step(weight, mean, square, gradient, factor, step_float):
    scaled = factor * gradient
    mean_new = beta_first * mean + (1.0 - beta_first) * scaled
    square_new = beta_second * square + (1.0 - beta_second) * scaled * scaled
    mean_hat = mean_new / (1.0 - jnp.power(beta_first, step_float))
    square_hat = square_new / (1.0 - jnp.power(beta_second, step_float))
    weight_new = weight - learn_rate * (
        mean_hat / (jnp.sqrt(square_hat) + adam_epsilon) + decay_rate * weight
    )
    return (weight_new, mean_new, square_new)


def body(
    attention_gradient,
    attention_weight,
    attention_mean,
    attention_square,
    expert_gradient,
    expert_weight,
    held_mean,
    held_square,
    live_block_count,
    holder_table,
    slot_table,
    step_count,
):
    local_gradient = attention_gradient[0]
    experts_all = holder_table.shape[0]
    per_holder = max(1, MAXB // lax.axis_size("expert"))
    block_position = jnp.arange(MAXB, dtype=jnp.int32)
    owner = lax.axis_index("expert")
    expert_pick = jnp.arange(experts_all, dtype=jnp.int32) == owner
    owned_block_count = jnp.sum(jnp.where(expert_pick, live_block_count, 0))
    own_holder = jnp.sum(jnp.where(expert_pick[:, None], holder_table, 0), axis=0)
    live_block_mask = block_position < owned_block_count
    gradient_tiles = expert_gradient[0, 0]
    expert_share = jnp.sum(
        jnp.where(live_block_mask[:, None], gradient_tiles * gradient_tiles, 0.0)
    )
    width = held_mean.shape[2]
    alive_all = block_position[None, :] < live_block_count[:, None]
    minelive = (holder_table == owner) & alive_all
    mine_count = minelive.astype(jnp.int32)
    rank_held = jnp.cumsum(mine_count, axis=1) - mine_count
    places = jnp.arange(per_holder, dtype=jnp.int32)
    slot_ids = jnp.arange(HSLOTS, dtype=jnp.int32)
    selector = jnp.sum(
        (
            minelive[:, :, None, None]
            & (rank_held[:, :, None, None] == places[None, None, :, None])
            & (slot_table[:, :, None, None] == slot_ids[None, None, None, :])
        ).astype(jnp.float32),
        axis=1,
    )
    outgoing_mean = jnp.einsum(
        "oqs,sd->oqd", selector, held_mean[0], precision=lax.Precision.HIGHEST
    )
    outgoing_square = jnp.einsum(
        "oqs,sd->oqd", selector, held_square[0], precision=lax.Precision.HIGHEST
    )
    incoming_mean, incoming_square = (
        lax.all_to_all(outgoing_mean, "expert", split_axis=0, concat_axis=0, tiled=True),
        lax.all_to_all(outgoing_square, "expert", split_axis=0, concat_axis=0, tiled=True),
    )
    earlier = (
        (own_holder[:, None] == own_holder[None, :])
        & live_block_mask[None, :]
        & (block_position[None, :] < block_position[:, None])
    )
    own_rank = jnp.sum(earlier.astype(jnp.int32), axis=1)
    target = own_holder * per_holder + own_rank
    flat_ids = jnp.arange(experts_all * per_holder, dtype=jnp.int32)
    picker = ((target[:, None] == flat_ids[None, :]) & live_block_mask[:, None]).astype(jnp.float32)
    owned_mean = jnp.dot(
        picker,
        incoming_mean.reshape(experts_all * per_holder, width),
        precision=lax.Precision.HIGHEST,
        preferred_element_type=jnp.float32,
    )
    owned_square = jnp.dot(
        picker,
        incoming_square.reshape(experts_all * per_holder, width),
        precision=lax.Precision.HIGHEST,
        preferred_element_type=jnp.float32,
    )
    owned_gradient = lax.psum_scatter(
        local_gradient.astype(jnp.float32), "dp", scatter_dimension=0, tiled=True
    )
    attention_part = jnp.sum(owned_gradient * owned_gradient)
    summed_parts = lax.psum((attention_part, expert_share), ("dp", "expert"))
    total = summed_parts[0] + summed_parts[1]
    factor = jnp.minimum(1.0, clip_norm / (jnp.sqrt(total) + 1e-06))
    step_float = step_count[0].astype(jnp.float32)
    attention_new, means_new, squares_new = adam_step(
        attention_weight, attention_mean, attention_square, owned_gradient, factor, step_float
    )
    weight_blocks = expert_weight[0, 0]
    weight_next, mean_next, square_next = adam_step(
        weight_blocks, owned_mean, owned_square, gradient_tiles, factor, step_float
    )
    live_flags = live_block_mask[:, None]
    experts_new = jnp.where(live_flags, weight_next, weight_blocks)
    means_kept = jnp.where(live_flags, mean_next, 0.0)
    squares_kept = jnp.where(live_flags, square_next, 0.0)
    return (
        attention_new,
        means_new,
        squares_new,
        experts_new[None, None],
        means_kept[None, None],
        squares_kept[None, None],
    )


def solution(mesh):
    placed = (
        P("dp", None, "expert"),
        P("dp", "expert"),
        P("dp", "expert"),
        P("dp", "expert"),
        P("dp", "expert", None, None),
        P("dp", "expert", None, None),
        P("dp", "expert", None),
        P("dp", "expert", None),
        P(),
        P(),
        P(),
        P(),
    )
    return jax.shard_map(
        body,
        mesh=mesh,
        in_specs=placed,
        out_specs=(
            P("dp", "expert"),
            P("dp", "expert"),
            P("dp", "expert"),
            P("dp", "expert", None, None),
            P("dp", "expert", None, None),
            P("dp", "expert", None, None),
        ),
        check_vma=False,
    )
```

profile of v0, /device:TPU:12, one launch (start us, length us, event | category | flops | bytes accessed | tf_op | source)
XLA Modules:
  0.0 139.0 jit_solution(14042447339251599127)
XLA Ops:
  7.2 0.0 copy-start
  7.2 0.0 copy-start.8
  7.2 0.0 copy-start.6
  7.2 0.0 copy-start.7
  7.2 0.0 copy-start.5
  7.2 0.0 reduce-scatter.2.cloned.1.call-start
  7.3 5.2 %bitcast_convert_fusion = f32[6144,256]{1,0:T(8,128)} fusion(bf16[1,6144,256]{2,1,0:T(8,128)(2,1)} %param.12), kind=kLoop, calls=%fused_computation.4 | loop fusion | flops 1572864 | bytes 9437184 | tf_op jit(solution)/shard_map/convert_element_type | solution.py:102
  12.5 0.0 copy-start.4
  12.5 0.0 copy-start.9
  12.5 0.0 copy-start.1
  12.5 0.0 copy-start.2
  12.5 0.0 copy-start.3
  12.5 0.0 reduce-scatter.2.cloned.1.call-update
  12.5 0.0 copy-done.8
  12.5 0.0 copy-done.6
  12.5 0.1 fusion.20
  12.6 0.2 reduce_window_sum.11
  12.8 0.0 copy-done.7
  12.8 0.1 iota_compare_fusion
  12.9 0.1 convert_reduce_fusion
  13.0 0.0 copy-done
  13.0 1.2 fusion.4
  14.2 4.2 %all-to-all-start.1 = ((f32[4,2,6144]{2,1,0:T(2,128)}), f32[4,2,6144]{2,1,0:T(2,128)S(1)}, u32[]{:S(2)}, u32[]{:S(2)}) async-start(f32[4,2,6144]{2,1,0:T(2,128)} %fusion.4), calls=%async_computation.2 | async-start | bytes 393216 | tf_op jit(solution)/shard_map/all_to_all | solution.py:78
  18.4 0.6 select_reduce_fusion.1
  19.1 0.7 iota_compare_fusion.5
  19.7 0.1 select_reduce_fusion
  19.8 0.2 convert_reduce_fusion.1
  20.0 0.0 copy-done.5
  20.0 1.2 fusion.6
  21.2 1.5 %all-to-all-done.1 = f32[4,2,6144]{2,1,0:T(2,128)S(1)} async-done(((f32[4,2,6144]{2,1,0:T(2,128)}), f32[4,2,6144]{2,1,0:T(2,128)S(1)}, u32[]{:S(2)}, u32[]{:S(2)}) %all-to-all-start.1) | async-done | bytes 196640 | tf_op jit(solution)/shard_map/all_to_all | solution.py:78
  22.7 4.3 %all-to-all-start = ((f32[4,2,6144]{2,1,0:T(2,128)}), f32[4,2,6144]{2,1,0:T(2,128)S(1)}, u32[]{:S(2)}, u32[]{:S(2)}) async-start(f32[4,2,6144]{2,1,0:T(2,128)} %fusion.6), calls=%async_computation.1 | async-start | bytes 393216 | tf_op jit(solution)/shard_map/all_to_all | solution.py:77
  27.0 0.0 copy-done.4
  27.0 0.7 fusion.10
  28.4 0.1 reshape.75
  28.6 52.3 %reduce-scatter.2.cloned.1.call-done = f32[768,256]{1,0:T(8,128)} async-done(((f32[6144,256]{1,0:T(8,128)}), f32[768,256]{1,0:T(8,128)}) %reduce-scatter.2.cloned.1.call-update) | async-done | bytes 786448 | tf_op jit(solution)/shard_map/reduce_scatter | solution.py:101
  80.8 1.9 %multiply_reduce_fusion = f32[]{:T(128)} fusion(f32[768,256]{1,0:T(8,128)} %reduce-scatter.2.cloned.1.call-done), kind=kLoop, calls=%fused_computation.9 | loop fusion | flops 393215 | bytes 786436 | tf_op jit(solution)/shard_map/reduce_sum | solution.py:104
  84.0 0.0 all-to-all-done
  84.1 0.1 reshape.74
  84.2 42.9 %psum.16 = f32[]{:T(128)} all-reduce(f32[]{:T(128)S(6)} %add.49), channel_id=1, replica_groups=mesh['dp'=8,'expert'=4] {'dp','expert'}, use_global_device_ids=true, to_apply=%region_2.3 | all-reduce | flops 1 | bytes 8 | tf_op jit(solution)/shard_map/psum | solution.py:105
  127.8 0.3 fusion
  128.1 0.0 copy-done.9
  128.1 1.1 select_bitcast_fusion
  129.2 0.0 copy-done.1
  129.2 0.0 copy-done.2
  129.2 0.0 copy-done.3
  129.2 2.9 %multiply_subtract_fusion = (f32[768,256]{1,0:T(8,128)}, f32[768,256]{1,0:T(8,128)}, f32[768,256]{1,0:T(8,128)}) fusion(f32[768,256]{1,0:T(8,128)S(1)} %copy-done.1, f32[]{:T(128)} %bitcast.3, f32[]{:T(128)} %bitcast.2, f32[768,256]{1,0:T(8,128)} %reduce-scatter.2.cloned.1.call-done, f32[]{:T(128)S(6)} %min.3, f32[768,256]{1,0:T(8,128)S(1)} %copy-done.2, ...), kind=kLoop, calls=%fused_computation.7 | loop fusion | flops 3145728 | bytes 5505036 | tf_op jit(solution)/shard_map/sub | solution.py:22
  (4 shorter events, 0.0 us)
Async XLA Ops:
  7.2 5.8 %copy-start = (f32[1,8,6144]{2,1,0:T(8,128)S(1)}, f32[1,8,6144]{2,1,0:T(8,128)}, u32[]{:S(2)}) copy-start(f32[1,8,6144]{2,1,0:T(8,128)} %param.19) | copy-start | bytes 589828
  7.2 5.3 %copy-start.8 = (s32[4]{0:T(128)S(1)}, s32[4]{0:T(128)}, u32[]{:S(2)}) copy-start(s32[4]{0:T(128)} %param.20) | copy-start | bytes 52
  7.2 5.3 %copy-start.6 = (s32[4,8]{1,0:T(4,128)S(1)}, s32[4,8]{1,0:T(4,128)}, u32[]{:S(2)}) copy-start(s32[4,8]{1,0:T(4,128)} %param.21) | copy-start | bytes 388
  7.2 5.6 %copy-start.7 = (s32[4,8]{1,0:T(4,128)S(1)}, s32[4,8]{1,0:T(4,128)}, u32[]{:S(2)}) copy-start(s32[4,8]{1,0:T(4,128)} %param.22) | copy-start | bytes 388
  7.2 12.8 %copy-start.5 = (f32[1,8,6144]{2,1,0:T(8,128)S(1)}, f32[1,8,6144]{2,1,0:T(8,128)}, u32[]{:S(2)}) copy-start(f32[1,8,6144]{2,1,0:T(8,128)} %param.18) | copy-start | bytes 589828
  7.2 73.6 %reduce-scatter.2.cloned.1.call-start = ((), (), s32[]{:S(2)}) async-start(), calls=%async_computation.3 | async-start | bytes 7077888 | tf_op jit(solution)/shard_map/reduce_scatter | solution.py:101
  12.5 14.5 %copy-start.4 = (f32[1,1,8,6144]{3,2,1,0:T(8,128)S(1)}, f32[1,1,8,6144]{3,2,1,0:T(8,128)}, u32[]{:S(2)}) copy-start(f32[1,1,8,6144]{3,2,1,0:T(8,128)} %param.16) | copy-start | bytes 589828
  12.5 115.6 %copy-start.9 = (f32[1,1,8,6144]{3,2,1,0:T(8,128)S(1)}, f32[1,1,8,6144]{3,2,1,0:T(8,128)}, u32[]{:S(2)}) copy-start(f32[1,1,8,6144]{3,2,1,0:T(8,128)} %param.17) | copy-start | bytes 589828
  12.5 116.8 %copy-start.1 = (f32[768,256]{1,0:T(8,128)S(1)}, f32[768,256]{1,0:T(8,128)}, u32[]{:S(2)}) copy-start(f32[768,256]{1,0:T(8,128)} %param.13) | copy-start | bytes 2359300
  12.5 116.8 %copy-start.2 = (f32[768,256]{1,0:T(8,128)S(1)}, f32[768,256]{1,0:T(8,128)}, u32[]{:S(2)}) copy-start(f32[768,256]{1,0:T(8,128)} %param.15) | copy-start | bytes 2359300
  12.5 116.8 %copy-start.3 = (f32[768,256]{1,0:T(8,128)S(1)}, f32[768,256]{1,0:T(8,128)}, u32[]{:S(2)}) copy-start(f32[768,256]{1,0:T(8,128)} %param.14) | copy-start | bytes 2359300
  14.2 8.5 %all-to-all-start.1 = ((f32[4,2,6144]{2,1,0:T(2,128)}), f32[4,2,6144]{2,1,0:T(2,128)S(1)}, u32[]{:S(2)}, u32[]{:S(2)}) async-start(f32[4,2,6144]{2,1,0:T(2,128)} %fusion.4), calls=%async_computation.2 | async-start | bytes 393216 | tf_op jit(solution)/shard_map/all_to_all | solution.py:78
  22.7 61.4 %all-to-all-start = ((f32[4,2,6144]{2,1,0:T(2,128)}), f32[4,2,6144]{2,1,0:T(2,128)S(1)}, u32[]{:S(2)}, u32[]{:S(2)}) async-start(f32[4,2,6144]{2,1,0:T(2,128)} %fusion.6), calls=%async_computation.1 | async-start | bytes 393216 | tf_op jit(solution)/shard_map/all_to_all | solution.py:77
Sparse Core Ops, SparseCore 0:
  12.6 68.1 reduce-scatter.1
where the time goes:
time: 139 us
  waiting for transfers between devices  53.7 us (39%)
  blocking collectives  42.9 us (31%)
  between operations  16.9 us (12%)
  other arithmetic  12.7 us (9%)
  starting transfers between devices  8.53 us (6%)
  matrix products  3.85 us (3%)
    reduce_scatter x1, waiting for transfers between devices, body(): lax.psum_scatter(local_gradient.astype(jnp.float32), 'dp', scatter_dimens...  52.3 us
    psum x1, blocking collectives, body(): summed_parts = lax.psum((attention_part, expert_share), ('dp', 'expert'))  42.9 us
    convert_element_type x1, other arithmetic, body(): local_gradient.astype(jnp.float32)  5.18 us
    all_to_all x1, starting transfers between devices, body(): lax.all_to_all(outgoing_mean, 'expert', split_axis=0, concat_axis=0, tile...  4.27 us
    all_to_all x1, starting transfers between devices, body(): lax.all_to_all(outgoing_square, 'expert', split_axis=0, concat_axis=0, ti...  4.22 us
    sub x1, other arithmetic, adam_step(): weight - learn_rate * (mean_hat / (jnp.sqrt(square_hat) + adam_epsilon) +...  2.9 us
  transfers between devices with their start and end apart: 3, of which 2 were waited for; matrix products, arithmetic and copies ran while one was open for 5% of the time, Pallas kernels for 0%

commit v1 on v0

--- a/solution.py
+++ b/solution.py
@@ -102,7 +102,7 @@
         local_gradient.astype(jnp.float32), "dp", scatter_dimension=0, tiled=True
     )
     attention_part = jnp.sum(owned_gradient * owned_gradient)
-    summed_parts = lax.psum((attention_part, expert_share), ("dp", "expert"))
+    summed_parts = lax.psum(lax.psum((attention_part, expert_share), "expert"), "dp")
     total = summed_parts[0] + summed_parts[1]
     factor = jnp.minimum(1.0, clip_norm / (jnp.sqrt(total) + 1e-06))
     step_float = step_count[0].astype(jnp.float32)

time: 139 us -> 126 us (0.906)
  the two profiles are of different devices: /device:TPU:12 before, /device:TPU:0 now
where the time goes in v1:
time: 126 us; the launch traced here: 125 us
  waiting for transfers between devices  58.2 us (46%)
  blocking collectives  24.5 us (19%)
  between operations  17 us (13%)
  other arithmetic  12.7 us (10%)
  starting transfers between devices  8.59 us (7%)
  matrix products  3.85 us (3%)
    reduce_scatter x1, waiting for transfers between devices, body(): lax.psum_scatter(local_gradient.astype(jnp.float32), 'dp', scatter_dimens...  55.8 us
    psum x1, blocking collectives, body(): lax.psum(lax.psum((attention_part, expert_share), 'expert'), 'dp')  14.2 us
    psum x1, blocking collectives, body(): lax.psum((attention_part, expert_share), 'expert')  10.3 us
    all_to_all x1, starting transfers between devices, body(): lax.all_to_all(outgoing_square, 'expert', split_axis=0, concat_axis=0, ti...  5.19 us
    convert_element_type x1, other arithmetic, body(): local_gradient.astype(jnp.float32)  5.18 us
    all_to_all x1, starting transfers between devices, body(): lax.all_to_all(outgoing_mean, 'expert', split_axis=0, concat_axis=0, tile...  3.37 us
    sub x1, other arithmetic, adam_step(): weight - learn_rate * (mean_hat / (jnp.sqrt(square_hat) + adam_epsilon) +...  2.9 us
  transfers between devices with their start and end apart: 3, of which 2 were waited for; matrix products, arithmetic and copies ran while one was open for 6% of the time, Pallas kernels for 0%

profile of v1, /device:TPU:0, one launch (start us, length us, event | category | flops | bytes accessed | tf_op | source)
XLA Modules:
  0.0 125.2 jit_solution(17172482204076333707)
XLA Ops:
  7.2 0.0 copy-start
  7.2 0.0 copy-start.8
  7.2 0.0 copy-start.6
  7.2 0.0 copy-start.7
  7.2 0.0 copy-start.5
  7.2 0.0 reduce-scatter.2.cloned.1.call-start
  7.3 5.2 %bitcast_convert_fusion = f32[6144,256]{1,0:T(8,128)} fusion(bf16[1,6144,256]{2,1,0:T(8,128)(2,1)} %param.12), kind=kLoop, calls=%fused_computation.4 | loop fusion | flops 1572864 | bytes 9437184 | tf_op jit(solution)/shard_map/convert_element_type | solution.py:102
  12.5 0.0 copy-start.4
  12.5 0.0 copy-start.9
  12.5 0.0 copy-start.1
  12.5 0.0 copy-start.2
  12.5 0.0 copy-start.3
  12.5 0.0 reduce-scatter.2.cloned.1.call-update
  12.5 0.0 copy-done.8
  12.5 0.0 copy-done.6
  12.5 0.1 fusion.20
  12.6 0.2 reduce_window_sum.11
  12.8 0.0 copy-done.7
  12.8 0.1 iota_compare_fusion
  12.9 0.1 convert_reduce_fusion
  13.0 0.0 copy-done
  13.0 1.2 fusion.4
  14.2 5.2 %all-to-all-start.1 = ((f32[4,2,6144]{2,1,0:T(2,128)}), f32[4,2,6144]{2,1,0:T(2,128)S(1)}, u32[]{:S(2)}, u32[]{:S(2)}) async-start(f32[4,2,6144]{2,1,0:T(2,128)} %fusion.4), calls=%async_computation.2 | async-start | bytes 393216 | tf_op jit(solution)/shard_map/all_to_all | solution.py:78
  19.4 0.6 select_reduce_fusion.1
  20.0 0.6 iota_compare_fusion.5
  20.7 0.1 select_reduce_fusion
  20.8 0.2 convert_reduce_fusion.1
  21.0 0.0 copy-done.5
  21.0 1.2 fusion.6
  22.2 2.4 %all-to-all-done.1 = f32[4,2,6144]{2,1,0:T(2,128)S(1)} async-done(((f32[4,2,6144]{2,1,0:T(2,128)}), f32[4,2,6144]{2,1,0:T(2,128)S(1)}, u32[]{:S(2)}, u32[]{:S(2)}) %all-to-all-start.1) | async-done | bytes 196640 | tf_op jit(solution)/shard_map/all_to_all | solution.py:78
  24.6 3.4 %all-to-all-start = ((f32[4,2,6144]{2,1,0:T(2,128)}), f32[4,2,6144]{2,1,0:T(2,128)S(1)}, u32[]{:S(2)}, u32[]{:S(2)}) async-start(f32[4,2,6144]{2,1,0:T(2,128)} %fusion.6), calls=%async_computation.1 | async-start | bytes 393216 | tf_op jit(solution)/shard_map/all_to_all | solution.py:77
  28.0 0.0 copy-done.4
  28.0 0.7 fusion.10
  29.4 55.8 %reduce-scatter.2.cloned.1.call-done = f32[768,256]{1,0:T(8,128)} async-done(((f32[6144,256]{1,0:T(8,128)}), f32[768,256]{1,0:T(8,128)}) %reduce-scatter.2.cloned.1.call-update) | async-done | bytes 786448 | tf_op jit(solution)/shard_map/reduce_scatter | solution.py:101
  85.2 1.9 %multiply_reduce_fusion = f32[]{:T(128)} fusion(f32[768,256]{1,0:T(8,128)} %reduce-scatter.2.cloned.1.call-done), kind=kLoop, calls=%fused_computation.9 | loop fusion | flops 393215 | bytes 786436 | tf_op jit(solution)/shard_map/reduce_sum | solution.py:104
  88.4 0.1 reshape.75
  88.6 10.3 %psum.33 = f32[]{:T(128)} all-reduce(f32[]{:T(128)S(6)} %add.53), channel_id=1, replica_groups=mesh['dp'=8,'expert'=4] {'expert'}, use_global_device_ids=true, to_apply=%region_2.3 | all-reduce | flops 1 | bytes 8 | tf_op jit(solution)/shard_map/psum | solution.py:105
  98.9 0.0 all-to-all-done
  98.9 0.1 reshape.74
  99.0 14.2 %psum.32 = f32[]{:T(128)} all-reduce(f32[]{:T(128)} %psum.33), channel_id=1, replica_groups=mesh['dp'=8,'expert'=4] {'dp'}, use_global_device_ids=true, to_apply=%region_3.4 | all-reduce | flops 1 | bytes 8 | tf_op jit(solution)/shard_map/psum | solution.py:105
  114.0 0.3 fusion
  114.3 0.0 copy-done.9
  114.3 1.1 select_bitcast_fusion
  115.4 0.0 copy-done.1
  115.4 0.0 copy-done.2
  115.4 0.0 copy-done.3
  115.4 2.9 %multiply_subtract_fusion = (f32[768,256]{1,0:T(8,128)}, f32[768,256]{1,0:T(8,128)}, f32[768,256]{1,0:T(8,128)}) fusion(f32[768,256]{1,0:T(8,128)S(1)} %copy-done.1, f32[]{:T(128)} %bitcast.3, f32[]{:T(128)} %bitcast.2, f32[768,256]{1,0:T(8,128)} %reduce-scatter.2.cloned.1.call-done, f32[]{:T(128)S(6)} %min.3, f32[768,256]{1,0:T(8,128)S(1)} %copy-done.2, ...), kind=kLoop, calls=%fused_computation.7 | loop fusion | flops 3145728 | bytes 5505036 | tf_op jit(solution)/shard_map/sub | solution.py:22
  (4 shorter events, 0.0 us)
Async XLA Ops:
  7.2 5.8 %copy-start = (f32[1,8,6144]{2,1,0:T(8,128)S(1)}, f32[1,8,6144]{2,1,0:T(8,128)}, u32[]{:S(2)}) copy-start(f32[1,8,6144]{2,1,0:T(8,128)} %param.19) | copy-start | bytes 589828
  7.2 5.3 %copy-start.8 = (s32[4]{0:T(128)S(1)}, s32[4]{0:T(128)}, u32[]{:S(2)}) copy-start(s32[4]{0:T(128)} %param.20) | copy-start | bytes 52
  7.2 5.3 %copy-start.6 = (s32[4,8]{1,0:T(4,128)S(1)}, s32[4,8]{1,0:T(4,128)}, u32[]{:S(2)}) copy-start(s32[4,8]{1,0:T(4,128)} %param.21) | copy-start | bytes 388
  7.2 5.6 %copy-start.7 = (s32[4,8]{1,0:T(4,128)S(1)}, s32[4,8]{1,0:T(4,128)}, u32[]{:S(2)}) copy-start(s32[4,8]{1,0:T(4,128)} %param.22) | copy-start | bytes 388
  7.2 13.8 %copy-start.5 = (f32[1,8,6144]{2,1,0:T(8,128)S(1)}, f32[1,8,6144]{2,1,0:T(8,128)}, u32[]{:S(2)}) copy-start(f32[1,8,6144]{2,1,0:T(8,128)} %param.18) | copy-start | bytes 589828
  7.2 78.0 %reduce-scatter.2.cloned.1.call-start = ((), (), s32[]{:S(2)}) async-start(), calls=%async_computation.3 | async-start | bytes 7077888 | tf_op jit(solution)/shard_map/reduce_scatter | solution.py:101
  12.5 15.5 %copy-start.4 = (f32[1,1,8,6144]{3,2,1,0:T(8,128)S(1)}, f32[1,1,8,6144]{3,2,1,0:T(8,128)}, u32[]{:S(2)}) copy-start(f32[1,1,8,6144]{3,2,1,0:T(8,128)} %param.16) | copy-start | bytes 589828
  12.5 101.8 %copy-start.9 = (f32[1,1,8,6144]{3,2,1,0:T(8,128)S(1)}, f32[1,1,8,6144]{3,2,1,0:T(8,128)}, u32[]{:S(2)}) copy-start(f32[1,1,8,6144]{3,2,1,0:T(8,128)} %param.17) | copy-start | bytes 589828
  12.5 103.0 %copy-start.1 = (f32[768,256]{1,0:T(8,128)S(1)}, f32[768,256]{1,0:T(8,128)}, u32[]{:S(2)}) copy-start(f32[768,256]{1,0:T(8,128)} %param.13) | copy-start | bytes 2359300
  12.5 103.0 %copy-start.2 = (f32[768,256]{1,0:T(8,128)S(1)}, f32[768,256]{1,0:T(8,128)}, u32[]{:S(2)}) copy-start(f32[768,256]{1,0:T(8,128)} %param.15) | copy-start | bytes 2359300
  12.5 103.0 %copy-start.3 = (f32[768,256]{1,0:T(8,128)S(1)}, f32[768,256]{1,0:T(8,128)}, u32[]{:S(2)}) copy-start(f32[768,256]{1,0:T(8,128)} %param.14) | copy-start | bytes 2359300
  14.2 10.4 %all-to-all-start.1 = ((f32[4,2,6144]{2,1,0:T(2,128)}), f32[4,2,6144]{2,1,0:T(2,128)S(1)}, u32[]{:S(2)}, u32[]{:S(2)}) async-start(f32[4,2,6144]{2,1,0:T(2,128)} %fusion.4), calls=%async_computation.2 | async-start | bytes 393216 | tf_op jit(solution)/shard_map/all_to_all | solution.py:78
  24.6 74.3 %all-to-all-start = ((f32[4,2,6144]{2,1,0:T(2,128)}), f32[4,2,6144]{2,1,0:T(2,128)S(1)}, u32[]{:S(2)}, u32[]{:S(2)}) async-start(f32[4,2,6144]{2,1,0:T(2,128)} %fusion.6), calls=%async_computation.1 | async-start | bytes 393216 | tf_op jit(solution)/shard_map/all_to_all | solution.py:77
Sparse Core Ops, SparseCore 0:
  12.6 72.5 reduce-scatter.1
